TPU v7x, 32 devices: a whole 2x2x4 slice. The times are simulated.
32 devices in a mesh: seq: 4 (over z), fsdp: 8 (over y, x, core).
Axes of the slice: x: 2, y: 2, z: 4, core: 2. Of those that a mesh axis runs over, the one named last changes fastest.
Arguments:
- tokens: float32 [16, 1024, 1536], P('fsdp', 'seq'), may hold values from -6 to 6
- cotangent: float32 [16, 1024, 1536], P('fsdp', 'seq'), may hold values from -6 to 6
- attention_gain: bfloat16 [1536], P('fsdp'), may hold values from 0.5 to 1.5
- feedforward_gain: bfloat16 [1536], P('fsdp'), may hold values from 0.5 to 1.5
- query_weight: bfloat16 [1536, 1536], P('fsdp'), may hold values from -1 to 1
- key_matrix: bfloat16 [1536, 768], P('fsdp'), may hold values from -16 to 16
- value_matrix: bfloat16 [1536, 768], P('fsdp'), may hold values from -0.15625 to 0.15625
- out_weight: bfloat16 [1536, 1536], P('fsdp'), may hold values from -1.25 to 1.25
- gate_weight: bfloat16 [1536, 4096], P('fsdp'), may hold values from -0.15625 to 0.15625
- up_weight: bfloat16 [1536, 4096], P('fsdp'), may hold values from -0.15625 to 0.15625
- down_weight: bfloat16 [4096, 1536], P('fsdp'), may hold values from -0.09375 to 0.09375
Outputs:
- block_out: float32 [16, 1024, 1536], P('fsdp', 'seq')
- grad_tokens: float32 [16, 1024, 1536], P('fsdp', 'seq')
- grad_attention_gain: float32 [1536], P('fsdp')
- grad_feedforward_gain: float32 [1536], P('fsdp')
- grad_query: float32 [1536, 1536], P('fsdp')
- grad_key: float32 [1536, 768], P('fsdp')
- grad_value: float32 [1536, 768], P('fsdp')
- grad_out: float32 [1536, 1536], P('fsdp')
- grad_gate: float32 [1536, 4096], P('fsdp')
- grad_up: float32 [1536, 4096], P('fsdp')
- grad_down: float32 [4096, 1536], P('fsdp')
All inputs are finite; a program needn't handle non-finite values.
Results may differ from a plain program's by a relative error of at most 0.024.
The roundings to bfloat16 on the way count: a program that leaves them out, or rounds other values in their place, can miss the bound.
Values may be sent and summed in bfloat16 or wider, within the bound.
A program may use at most 320 MiB of HBM per device.

v0:
```python
from functools import partial
import math
import jax
import jax.numpy as jnp
from jax import lax
from jax.sharding import PartitionSpec as P

QUERY_HEADS = 16
KEY_VALUE_HEADS = 8
HEAD_DIM = 96
norm_eps = 1e-05
rope_base = 100000.0
masked_score = -1e30


def rope_tables(positions, head_size):
    half = head_size // 2
    freqs = rope_base ** (-(2.0 * jnp.arange(half, dtype=jnp.float32)) / head_size)
    angles = positions.astype(jnp.float32)[:, None] * freqs[None, :]
    return (jnp.cos(angles), jnp.sin(angles))


def rotate_halves(values, cosine, sine):
    half = values.shape[-1] // 2
    first = values[..., :half]
    second = values[..., half:]
    return jnp.concatenate(
        [first * cosine - second * sine, second * cosine + first * sine], axis=-1
    )


def reverse_rotation(grads, cosine, sine):
    half = grads.shape[-1] // 2
    first = grads[..., :half]
    second = grads[..., half:]
    return jnp.concatenate(
        [first * cosine + second * sine, second * cosine - first * sine], axis=-1
    )


def masked_scores(query_rows, key_rows, scale):
    sequence_length = query_rows.shape[0]
    scores = (
        jnp.einsum("qhgd,khd->hgqk", query_rows, key_rows, preferred_element_type=jnp.float32)
        * scale
    )
    causal = jnp.arange(sequence_length)[:, None] >= jnp.arange(sequence_length)[None, :]
    return jnp.where(causal, scores, masked_score)


def attend_items(packed_arrays, group_size, head_size):
    count, sequence_length, features = packed_arrays.shape
    kv_local = features // ((group_size + 2) * head_size)
    scale = 1.0 / math.sqrt(head_size)

    def single(item):
        split = item.reshape(sequence_length, kv_local, group_size + 2, head_size)
        query_rows = split[:, :, :group_size, :]
        key_rows = split[:, :, group_size, :]
        value_matrix_rows = split[:, :, group_size + 1, :]
        scores = masked_scores(query_rows, key_rows, scale)
        top_score = jnp.max(scores, axis=-1, keepdims=True)
        log_total = top_score + jnp.log(
            jnp.sum(jnp.exp(scores - top_score), axis=-1, keepdims=True)
        )
        probs = jnp.exp(scores - log_total).astype(jnp.bfloat16)
        attended = jnp.einsum(
            "hgqk,khd->qhgd", probs, value_matrix_rows, preferred_element_type=jnp.float32
        )
        return (
            attended.astype(jnp.bfloat16).reshape(
                sequence_length, kv_local * group_size * head_size
            ),
            log_total[..., 0],
        )

    attended_all, log_totals = lax.map(single, packed_arrays)
    return (attended_all, log_totals, packed_arrays)


def attend_back_item(inputs, group_size, head_size, cosine, sine):
    packed_item, attended_item, log_total, grad_item = inputs
    sequence_length = packed_item.shape[0]
    kv_local = packed_item.shape[1] // ((group_size + 2) * head_size)
    scale = 1.0 / math.sqrt(head_size)
    split = packed_item.reshape(sequence_length, kv_local, group_size + 2, head_size)
    query_rows = split[:, :, :group_size, :]
    key_rows = split[:, :, group_size, :]
    value_matrix_rows = split[:, :, group_size + 1, :]
    out_heads = attended_item.reshape(sequence_length, kv_local, group_size, head_size)
    grad_heads = grad_item.reshape(sequence_length, kv_local, group_size, head_size)
    scores = masked_scores(query_rows, key_rows, scale)
    probs = jnp.exp(scores - log_total[..., None])
    delta = jnp.einsum("qhgd,qhgd->hgq", grad_heads, out_heads, preferred_element_type=jnp.float32)
    value_gradients = jnp.einsum(
        "hgqk,qhgd->khd", probs.astype(jnp.bfloat16), grad_heads, preferred_element_type=jnp.float32
    )
    grad_probs = jnp.einsum(
        "qhgd,khd->hgqk", grad_heads, value_matrix_rows, preferred_element_type=jnp.float32
    )
    grad_scores = (probs * (grad_probs - delta[..., None]) * scale).astype(jnp.bfloat16)
    grad_queries = jnp.einsum(
        "hgqk,khd->qhgd", grad_scores, key_rows, preferred_element_type=jnp.float32
    )
    key_gradients = jnp.einsum(
        "hgqk,qhgd->khd", grad_scores, query_rows, preferred_element_type=jnp.float32
    )
    grad_queries = reverse_rotation(grad_queries, cosine[:, None, None, :], sine[:, None, None, :])
    key_gradients = reverse_rotation(key_gradients, cosine[:, None, :], sine[:, None, :])
    stacked = jnp.concatenate(
        [
            grad_queries.astype(jnp.bfloat16),
            key_gradients.astype(jnp.bfloat16)[:, :, None, :],
            value_gradients.astype(jnp.bfloat16)[:, :, None, :],
        ],
        axis=2,
    )
    return stacked.reshape(sequence_length, kv_local * (group_size + 2) * head_size)


def norm_back(grad_normed, normed, inverse, gain):
    scaled = grad_normed * gain
    return inverse * (scaled - normed * jnp.mean(scaled * normed, axis=-1, keepdims=True))


def body(
    tokens,
    cotangent,
    attention_gain,
    feedforward_gain,
    query_weight,
    key_matrix,
    value_matrix,
    out_weight,
    gate_weight,
    up_weight,
    down_weight,
):
    sequence_count, span_length, width = tokens.shape
    row_count = sequence_count * span_length
    group_size = QUERY_HEADS // KEY_VALUE_HEADS
    gain_low_one, gain_low_two, whole_query, whole_key, whole_value, whole_out = (
        lax.all_gather(attention_gain, "fsdp", axis=0, tiled=True),
        lax.all_gather(feedforward_gain, "fsdp", axis=0, tiled=True),
        lax.all_gather(query_weight, "fsdp", axis=0, tiled=True),
        lax.all_gather(key_matrix, "fsdp", axis=0, tiled=True),
        lax.all_gather(value_matrix, "fsdp", axis=0, tiled=True),
        lax.all_gather(out_weight, "fsdp", axis=0, tiled=True),
    )
    gain_one = gain_low_one.astype(jnp.float32)
    gain_two = gain_low_two.astype(jnp.float32)
    positions = lax.axis_index("seq") * span_length + jnp.arange(span_length, dtype=jnp.int32)
    cosine, sine = rope_tables(positions, HEAD_DIM)
    cosine_rows = jnp.tile(cosine, (sequence_count, 1))[:, None, :]
    sine_rows = jnp.tile(sine, (sequence_count, 1))[:, None, :]
    flat = tokens.reshape(row_count, width)
    inv_one = lax.rsqrt(jnp.mean(flat * flat, axis=-1, keepdims=True) + norm_eps)
    normed_one = flat * inv_one
    first_inputs = (normed_one * gain_one).astype(jnp.bfloat16)
    query_projected = jnp.dot(
        first_inputs, whole_query, preferred_element_type=jnp.float32
    ).reshape(row_count, QUERY_HEADS, HEAD_DIM)
    key_projected = jnp.dot(first_inputs, whole_key, preferred_element_type=jnp.float32).reshape(
        row_count, KEY_VALUE_HEADS, HEAD_DIM
    )
    value_matrix_rows = jnp.dot(
        first_inputs, whole_value, preferred_element_type=jnp.float32
    ).astype(jnp.bfloat16)
    query_rotated = (
        rotate_halves(query_projected, cosine_rows, sine_rows)
        .astype(jnp.bfloat16)
        .reshape(row_count, KEY_VALUE_HEADS, group_size, HEAD_DIM)
    )
    key_rotated = (
        rotate_halves(key_projected, cosine_rows, sine_rows)
        .astype(jnp.bfloat16)
        .reshape(row_count, KEY_VALUE_HEADS, 1, HEAD_DIM)
    )
    packed_arrays = jnp.concatenate(
        [
            query_rotated,
            key_rotated,
            value_matrix_rows.reshape(row_count, KEY_VALUE_HEADS, 1, HEAD_DIM),
        ],
        axis=2,
    )
    packed_arrays = packed_arrays.reshape(
        sequence_count, span_length, KEY_VALUE_HEADS * (group_size + 2) * HEAD_DIM
    )
    attend_fn = partial(attend_items, group_size=group_size, head_size=HEAD_DIM)
    heads_attended, log_totals, head_inputs = attend_fn(
        lax.all_to_all(packed_arrays, "seq", split_axis=2, concat_axis=1, tiled=True)
    )
    attended_flat = lax.all_to_all(
        heads_attended, "seq", split_axis=1, concat_axis=2, tiled=True
    ).reshape(row_count, QUERY_HEADS * HEAD_DIM)
    hidden_one = flat + jnp.dot(attended_flat, whole_out, preferred_element_type=jnp.float32)
    inv_two = lax.rsqrt(jnp.mean(hidden_one * hidden_one, axis=-1, keepdims=True) + norm_eps)
    normed_two = hidden_one * inv_two
    inputs_two = (normed_two * gain_two).astype(jnp.bfloat16)
    pieces = (
        lax.all_gather(gate_weight, "fsdp", axis=0, tiled=True),
        lax.all_gather(up_weight, "fsdp", axis=0, tiled=True),
    )
    columns = inputs_two
    gate_pre = jnp.dot(columns, pieces[0], preferred_element_type=jnp.float32)
    up_pre = jnp.dot(columns, pieces[1], preferred_element_type=jnp.float32)
    sigmoid_gate = jax.nn.sigmoid(gate_pre)
    hidden_act = (gate_pre * sigmoid_gate * up_pre).astype(jnp.bfloat16)
    columns = hidden_act
    ffn_result = jnp.dot(
        columns,
        lax.all_gather(down_weight, "fsdp", axis=0, tiled=True),
        preferred_element_type=jnp.float32,
    )
    block_out = hidden_one + ffn_result
    grad_flat = cotangent.reshape(row_count, width)
    grad_low = grad_flat.astype(jnp.bfloat16)
    grad_down = jnp.dot(hidden_act.T, grad_low, preferred_element_type=jnp.float32)
    grad_hidden = jnp.dot(
        grad_low,
        lax.all_gather(down_weight, "fsdp", axis=0, tiled=True).T,
        preferred_element_type=jnp.float32,
    )
    grad_gate_pre = (
        grad_hidden * up_pre * sigmoid_gate * (1.0 + gate_pre * (1.0 - sigmoid_gate))
    ).astype(jnp.bfloat16)
    grad_up_pre = (grad_hidden * gate_pre * sigmoid_gate).astype(jnp.bfloat16)
    grad_gate = jnp.dot(inputs_two.T, grad_gate_pre, preferred_element_type=jnp.float32)
    grad_up = jnp.dot(inputs_two.T, grad_up_pre, preferred_element_type=jnp.float32)
    pieces = (
        lax.all_gather(gate_weight, "fsdp", axis=0, tiled=True),
        lax.all_gather(up_weight, "fsdp", axis=0, tiled=True),
    )
    block = jnp.dot(grad_gate_pre, pieces[0].T, preferred_element_type=jnp.float32) + jnp.dot(
        grad_up_pre, pieces[1].T, preferred_element_type=jnp.float32
    )
    gain_grad_two = jnp.sum(block * normed_two, axis=0)
    grad_hidden_one = grad_flat + norm_back(block, normed_two, inv_two, gain_two)
    ffn_shards = (
        lax.psum_scatter(
            gain_grad_two.astype(jnp.bfloat16), "fsdp", scatter_dimension=0, tiled=True
        ).astype(jnp.float32),
        lax.psum_scatter(
            grad_gate.astype(jnp.bfloat16), "fsdp", scatter_dimension=0, tiled=True
        ).astype(jnp.float32),
        lax.psum_scatter(
            grad_up.astype(jnp.bfloat16), "fsdp", scatter_dimension=0, tiled=True
        ).astype(jnp.float32),
        lax.psum_scatter(
            grad_down.astype(jnp.bfloat16), "fsdp", scatter_dimension=0, tiled=True
        ).astype(jnp.float32),
    )
    grad_low_one = grad_hidden_one.astype(jnp.bfloat16)
    grad_out_w = jnp.dot(attended_flat.T, grad_low_one, preferred_element_type=jnp.float32)
    attended_gradient = jnp.dot(
        grad_low_one, whole_out.T, preferred_element_type=jnp.float32
    ).astype(jnp.bfloat16)
    attended_gradient = attended_gradient.reshape(
        sequence_count, span_length, QUERY_HEADS * HEAD_DIM
    )
    grad_heads = lax.all_to_all(attended_gradient, "seq", split_axis=2, concat_axis=1, tiled=True)
    full_len = grad_heads.shape[1]
    full_cos, full_sin = rope_tables(jnp.arange(full_len, dtype=jnp.int32), HEAD_DIM)
    back_fn = partial(
        attend_back_item, group_size=group_size, head_size=HEAD_DIM, cosine=full_cos, sine=full_sin
    )
    packed_grads = lax.map(back_fn, (head_inputs, heads_attended, log_totals, grad_heads))
    token_gradients = lax.all_to_all(
        packed_grads, "seq", split_axis=1, concat_axis=2, tiled=True
    ).reshape(row_count, KEY_VALUE_HEADS, group_size + 2, HEAD_DIM)
    grad_queries = token_gradients[:, :, :group_size, :].reshape(row_count, QUERY_HEADS * HEAD_DIM)
    key_gradients = token_gradients[:, :, group_size, :].reshape(
        row_count, KEY_VALUE_HEADS * HEAD_DIM
    )
    value_gradients = token_gradients[:, :, group_size + 1, :].reshape(
        row_count, KEY_VALUE_HEADS * HEAD_DIM
    )
    grad_query = jnp.dot(first_inputs.T, grad_queries, preferred_element_type=jnp.float32)
    grad_key = jnp.dot(first_inputs.T, key_gradients, preferred_element_type=jnp.float32)
    grad_value = jnp.dot(first_inputs.T, value_gradients, preferred_element_type=jnp.float32)
    grad_inputs_one = (
        jnp.dot(grad_queries, whole_query.T, preferred_element_type=jnp.float32)
        + jnp.dot(key_gradients, whole_key.T, preferred_element_type=jnp.float32)
        + jnp.dot(value_gradients, whole_value.T, preferred_element_type=jnp.float32)
    )
    gain_grad_one = jnp.sum(grad_inputs_one * normed_one, axis=0)
    grad_tokens = grad_hidden_one + norm_back(grad_inputs_one, normed_one, inv_one, gain_one)
    attn_shards = (
        lax.psum_scatter(
            gain_grad_one.astype(jnp.bfloat16), "fsdp", scatter_dimension=0, tiled=True
        ).astype(jnp.float32),
        lax.psum_scatter(
            grad_query.astype(jnp.bfloat16), "fsdp", scatter_dimension=0, tiled=True
        ).astype(jnp.float32),
        lax.psum_scatter(
            grad_key.astype(jnp.bfloat16), "fsdp", scatter_dimension=0, tiled=True
        ).astype(jnp.float32),
        lax.psum_scatter(
            grad_value.astype(jnp.bfloat16), "fsdp", scatter_dimension=0, tiled=True
        ).astype(jnp.float32),
        lax.psum_scatter(
            grad_out_w.astype(jnp.bfloat16), "fsdp", scatter_dimension=0, tiled=True
        ).astype(jnp.float32),
    )
    summed = (
        lax.psum(attn_shards[0].astype(jnp.bfloat16), "seq").astype(jnp.float32),
        lax.psum(ffn_shards[0].astype(jnp.bfloat16), "seq").astype(jnp.float32),
        lax.psum(attn_shards[1].astype(jnp.bfloat16), "seq").astype(jnp.float32),
        lax.psum(attn_shards[2].astype(jnp.bfloat16), "seq").astype(jnp.float32),
        lax.psum(attn_shards[3].astype(jnp.bfloat16), "seq").astype(jnp.float32),
        lax.psum(attn_shards[4].astype(jnp.bfloat16), "seq").astype(jnp.float32),
        lax.psum(ffn_shards[1].astype(jnp.bfloat16), "seq").astype(jnp.float32),
        lax.psum(ffn_shards[2].astype(jnp.bfloat16), "seq").astype(jnp.float32),
        lax.psum(ffn_shards[3].astype(jnp.bfloat16), "seq").astype(jnp.float32),
    )
    return (
        block_out.reshape(sequence_count, span_length, width),
        grad_tokens.reshape(sequence_count, span_length, width),
        summed[0],
        summed[1],
        summed[2],
        summed[3],
        summed[4],
        summed[5],
        summed[6],
        summed[7],
        summed[8],
    )


def solution(mesh):
    placed = (
        P("fsdp", "seq", None),
        P("fsdp", "seq", None),
        P("fsdp"),
        P("fsdp"),
        P("fsdp", None),
        P("fsdp", None),
        P("fsdp", None),
        P("fsdp", None),
        P("fsdp", None),
        P("fsdp", None),
        P("fsdp", None),
    )
    return jax.shard_map(
        body,
        mesh=mesh,
        in_specs=placed,
        out_specs=(
            P("fsdp", "seq", None),
            P("fsdp", "seq", None),
            P("fsdp"),
            P("fsdp"),
            P("fsdp", None),
            P("fsdp", None),
            P("fsdp", None),
            P("fsdp", None),
            P("fsdp", None),
            P("fsdp", None),
            P("fsdp", None),
        ),
        check_vma=False,
    )
```

profile of v0, /device:TPU:0, one launch (start us, length us, event | category | flops | bytes accessed | tf_op | source)
XLA Modules:
  0.0 1337.4 jit_solution(4431075528565036426)
XLA Ops:
  13.8 15.5 %all-reduce.5 = (bf16[1536]{0:T(1024)(128)(2,1)S(1)}, bf16[1536]{0:T(1024)(128)(2,1)S(1)}) all-reduce(bf16[1536]{0:T(1024)(128)(2,1)S(1)} %dynamic-update-slice, bf16[1536]{0:T(1024)(128)(2,1)S(1)} %dynamic-update-slice.1), channel_id=1, replica_groups=mesh['seq'=4,'fsdp'=8] {'fsdp'}, use_global_device_ids=true, to_apply=%add | all-reduce | flops 3072 | bytes 12288
  33.0 8.7 all-gather.10.cloned.1.call-done
  48.5 24.0 %all-gather.12.cloned.1.call-done = bf16[1536,768]{1,0:T(8,128)(2,1)} async-done(((bf16[192,768]{1,0:T(8,128)(2,1)}), bf16[1536,768]{1,0:T(8,128)(2,1)}) %all-gather.12.cloned.1.call-update) | async-done | bytes 2359312 | tf_op jit(solution)/shard_map/all_gather | solution.py:147
  78.4 34.8 %all-gather.8.cloned.1.call-done = bf16[1536,1536]{1,0:T(8,128)(2,1)} async-done(((bf16[192,1536]{1,0:T(8,128)(2,1)}), bf16[1536,1536]{1,0:T(8,128)(2,1)}) %all-gather.8.cloned.1.call-update) | async-done | bytes 4718608 | tf_op jit(solution)/shard_map/all_gather | solution.py:145
  134.1 71.1 %all-to-all-done = bf16[2,256,3072]{1,0,2:T(2,128)(2,1)S(1)} async-done(((bf16[2,256,3072]{1,0,2:T(2,128)(2,1)}), bf16[2,256,3072]{1,0,2:T(2,128)(2,1)S(1)}, u32[]{:S(2)}, u32[]{:S(2)}) %all-to-all-start) | async-done | bytes 3145760 | tf_op jit(solution)/shard_map/all_to_all | solution.py:192
  215.1 29.1 %while.25 = (s32[]{:T(128)}, bf16[2,1024,384]{1,2,0:T(8,128)(2,1)}, f32[2,2,2,1024]{3,2,1,0:T(2,128)S(1)}, bf16[2,1024,768]{1,2,0:T(8,128)(2,1)S(1)}, s32[]{:T(128)}) while((s32[]{:T(128)}, bf16[2,1024,384]{1,2,0:T(8,128)(2,1)}, f32[2,2,2,1024]{3,2,1,0:T(2,128)S(1)}, bf16[2,1024,768]{1,2,0:T(8,128)(2,1)S(1)}, s32[]{:T(128)}) %tuple.80), condition=%wide.region_4.5_spmd, body=%wide.region_1.4_spmd.sunk | while | flops 1658187776 | bytes 68026976 | solution.py:77
  256.9 33.5 %all-to-all-done.1 = bf16[2,1024,384]{2,0,1:T(2,128)(2,1)} async-done(((bf16[2,1024,384]{2,0,1:T(2,128)(2,1)}), bf16[2,1024,384]{2,0,1:T(2,128)(2,1)}, u32[]{:S(2)}, u32[]{:S(2)}) %all-to-all-start.1) | async-done | bytes 1572896 | tf_op jit(solution)/shard_map/all_to_all | solution.py:194
  304.1 12.1 fusion.46
  316.2 12.2 fusion.47
  328.4 46.9 %all-gather.20.cloned.1.call-done = bf16[4096,1536]{1,0:T(8,128)(2,1)} async-done(((bf16[512,1536]{1,0:T(8,128)(2,1)}), bf16[4096,1536]{1,0:T(8,128)(2,1)}) %all-gather.20.cloned.1.call-update) | async-done | bytes 12582928 | tf_op jit(solution)/shard_map/all_gather | solution.py:213
  375.2 19.2 %multiply_convert_fusion = (bf16[512,4096]{1,0:T(8,128)(2,1)}, bf16[512,4096]{1,0:T(8,128)(2,1)}, bf16[512,4096]{1,0:T(8,128)(2,1)}) fusion(f32[512,4096]{1,0:T(8,128)} %fusion.46, f32[512,4096]{1,0:T(8,128)} %fusion.47, bf16[512,1536]{1,0:T(8,128)(2,1)} %bitcast_convert_fusion, bf16[4096,1536]{1,0:T(8,128)(2,1)} %all-gather.20.cloned.1.call-done), kind=kOutput, calls=%fused_computation.61 | convolution fusion | flops 6476005376 | bytes 43515904 | tf_op jit(solution)/shard_map/dot_general | solution.py:220
  394.4 11.2 fusion.48
  405.7 12.0 multiply_reduce_fusion
  442.4 30.3 %all-to-all-done.2 = bf16[2,256,1536]{1,0,2:T(2,128)(2,1)} async-done(((bf16[2,256,1536]{1,0,2:T(2,128)(2,1)}), bf16[2,256,1536]{1,0,2:T(2,128)(2,1)}, u32[]{:S(2)}, u32[]{:S(2)}) %all-to-all-start.2) | async-done | bytes 1572896 | tf_op jit(solution)/shard_map/all_to_all | solution.py:262
  480.3 73.4 %while.26 = (s32[]{:T(128)}, bf16[2,1024,768]{1,2,0:T(8,128)(2,1)}, bf16[2,1024,768]{1,2,0:T(8,128)(2,1)S(1)}, f32[2,2,2,1024]{3,2,1,0:T(2,128)S(1)}, bf16[2,102...) while((s32[]{:T(128)}, bf16[2,1024,768]{1,2,0:T(8,128)(2,1)}, ...), condition=%wide.region_8.9_spmd.clone.clone.clone, body=%wide.region_7.8_spmd.clone.clone.clone.sunk | while | flops 4085755904 | bytes 115446648 | solution.py:268
  482.4 8.3 fusion.118
  491.0 10.1 fusion.121
  527.4 10.0 fusion.121
  561.3 73.6 %all_to_all.66 = bf16[2,1024,768]{2,0,1:T(2,128)(2,1)} all-to-all(bf16[2,1024,768]{2,0,1:T(2,128)(2,1)S(1)} %copy.81), channel_id=1, replica_groups=mesh['seq'=4,'fsdp'=8] {'seq'}, dimensions={1} | all-to-all | bytes 6291456 | tf_op jit(solution)/shard_map/all_to_all | solution.py:269
  634.9 11.2 copy.82
  667.9 11.8 convolution_convert_fusion.2
  679.8 11.9 convolution_convert_fusion.1
  693.1 11.9 convolution_convert_fusion
  705.1 37.1 %reduce-scatter.12.cloned.1.call-done = bf16[192,768]{1,0:T(8,128)(2,1)} async-done(((bf16[1536,768]{1,0:T(8,128)(2,1)}), bf16[192,768]{1,0:T(8,128)(2,1)}) %reduce-scatter.12.cloned.1.call-update) | async-done | bytes 294928 | tf_op jit(solution)/shard_map/reduce_scatter | solution.py:299
  742.2 57.3 %reduce-scatter.8.cloned.1.call-done = bf16[192,1536]{1,0:T(8,128)(2,1)} async-done(((bf16[1536,1536]{1,0:T(8,128)(2,1)}), bf16[192,1536]{1,0:T(8,128)(2,1)}) %reduce-scatter.8.cloned.1.call-update) | async-done | bytes 589840 | tf_op jit(solution)/shard_map/reduce_scatter | solution.py:293
  799.5 95.7 %reduce-scatter.16.cloned.1.call-done = bf16[192,4096]{1,0:T(8,128)(2,1)} async-done(((bf16[1536,4096]{1,0:T(8,128)(2,1)}), bf16[192,4096]{1,0:T(8,128)(2,1)}) %reduce-scatter.16.cloned.1.call-update) | async-done | bytes 1572880 | tf_op jit(solution)/shard_map/reduce_scatter | solution.py:244
  895.2 95.8 %reduce-scatter.18.cloned.1.call-done = bf16[192,4096]{1,0:T(8,128)(2,1)} async-done(((bf16[1536,4096]{1,0:T(8,128)(2,1)}), bf16[192,4096]{1,0:T(8,128)(2,1)}) %reduce-scatter.18.cloned.1.call-update) | async-done | bytes 1572880 | tf_op jit(solution)/shard_map/reduce_scatter | solution.py:247
  991.0 95.7 %reduce-scatter.20.cloned.1.call-done = bf16[512,1536]{1,0:T(8,128)(2,1)} async-done(((bf16[4096,1536]{1,0:T(8,128)(2,1)}), bf16[512,1536]{1,0:T(8,128)(2,1)}) %reduce-scatter.20.cloned.1.call-update) | async-done | bytes 1572880 | tf_op jit(solution)/shard_map/reduce_scatter | solution.py:250
  1088.5 12.2 convolution_add_fusion.3
  1112.1 13.6 %all-reduce.4 = (bf16[1536]{0:T(1024)(128)(2,1)S(1)}, bf16[1536]{0:T(1024)(128)(2,1)S(1)}) all-reduce(bf16[1536]{0:T(1024)(128)(2,1)S(1)} %get-tuple-element.208, bf16[1536]{0:T(1024)(128)(2,1)S(1)} %copy-done.38), channel_id=2, replica_groups=mesh['seq'=4,'fsdp'=8] {'fsdp'}, use_global_device_ids=true, to_apply=%region_11.12.clone | all-reduce | flops 3072 | bytes 12288
  1125.8 12.3 all-reduce.6
  1144.5 174.5 %all-reduce.10.cloned.1.call-done = (bf16[192,1536]{1,0:T(8,128)(2,1)}, bf16[192,768]{1,0:T(8,128)(2,1)}, bf16[192,768]{1,0:T(8,128)(2,1)}, bf16[192,1536]{1,0:T...) async-done(((bf16[192,1536]{1,0:T(8,128)(2,1)}, bf16[192,768]{1,0:T(8,128)(2,1)}, bf16[192,768]{1,0:T(8,128)(2,1)}, ...) | async-done | bytes 6488080 | tf_op jit(solution)/shard_map/psum | solution.py:309
  (245 shorter events, 246.1 us)
Async XLA Ops:
  7.2 34.6 %all-gather.10.cloned.1.call-start = ((), (), s32[]{:S(2)}) async-start(), calls=%async_computation.12 | async-start | bytes 2654208 | tf_op jit(solution)/shard_map/all_gather | solution.py:146
  7.9 5.6 copy-start.41
  7.9 21.4 %copy-start = (f32[2,256,1536]{2,1,0:T(8,128)S(1)}, f32[2,256,1536]{2,1,0:T(8,128)}, u32[]{:S(2)}) copy-start(f32[2,256,1536]{2,1,0:T(8,128)} %param.15) | copy-start | bytes 9437188
  8.0 64.6 %all-gather.12.cloned.1.call-start = ((), (), s32[]{:S(2)}) async-start(), calls=%async_computation.13 | async-start | bytes 2654208 | tf_op jit(solution)/shard_map/all_gather | solution.py:147
  8.7 104.5 %all-gather.8.cloned.1.call-start = ((), (), s32[]{:S(2)}) async-start(), calls=%async_computation.11 | async-start | bytes 5308416 | tf_op jit(solution)/shard_map/all_gather | solution.py:145
  9.4 285.0 %all-gather.14.cloned.1.call-start = ((), (), s32[]{:S(2)}) async-start(), calls=%async_computation.14 | async-start | bytes 5308416 | tf_op jit(solution)/shard_map/all_gather | solution.py:148
  10.0 294.1 %all-gather.16.cloned.1.call-start = ((), (), s32[]{:S(2)}) async-start(), calls=%async_computation.15 | async-start | bytes 14155776 | tf_op jit(solution)/shard_map/all_gather | solution.py:202
  10.6 305.6 %all-gather.18.cloned.1.call-start = ((), (), s32[]{:S(2)}) async-start(), calls=%async_computation.16 | async-start | bytes 14155776 | tf_op jit(solution)/shard_map/all_gather | solution.py:203
  11.2 364.1 %all-gather.20.cloned.1.call-start = ((), (), s32[]{:S(2)}) async-start(), calls=%async_computation.17 | async-start | bytes 14155776 | tf_op jit(solution)/shard_map/all_gather | solution.py:213
  12.0 18.0 %copy-start.36 = (f32[48]{0:T(128)}, f32[48]{0:T(128)S(1)}, u32[]{:S(2)}) copy-start(f32[48]{0:T(128)S(1)} %multiply_power_fusion) | copy-start | bytes 580
  48.5 28.7 %copy-start.20 = (f32[512,8,96]{0,2,1:T(8,128)S(1)}, f32[512,8,96]{0,2,1:T(8,128)}, u32[]{:S(2)}) copy-start(f32[512,8,96]{0,2,1:T(8,128)} %fusion.45) | copy-start | bytes 4718596
  113.2 6.8 copy-start.21
  129.3 75.8 %all-to-all-start = ((bf16[2,256,3072]{1,0,2:T(2,128)(2,1)}), bf16[2,256,3072]{1,0,2:T(2,128)(2,1)S(1)}, u32[]{:S(2)}, u32[]{:S(2)}) async-start(bf16[2,256,3072]{1,0,2:T(2,128)(2,1)} %reshape.346), calls=%async_computation | async-start | bytes 6291456 | tf_op jit(solution)/shard_map/all_to_all | solution.py:192
  249.1 41.3 %all-to-all-start.1 = ((bf16[2,1024,384]{2,0,1:T(2,128)(2,1)}), bf16[2,1024,384]{2,0,1:T(2,128)(2,1)}, u32[]{:S(2)}, u32[]{:S(2)}) async-start(bf16[2,1024,384]{2,0,1:T(2,128)(2,1)} %copy.76), calls=%async_computation.1 | async-start | bytes 3145728 | tf_op jit(solution)/shard_map/all_to_all | solution.py:194
  394.4 11.2 copy-start.9
  405.6 12.0 copy-start.6
  418.4 7.3 copy-start.7
  430.6 42.1 %all-to-all-start.2 = ((bf16[2,256,1536]{1,0,2:T(2,128)(2,1)}), bf16[2,256,1536]{1,0,2:T(2,128)(2,1)}, u32[]{:S(2)}, u32[]{:S(2)}) async-start(bf16[2,256,1536]{1,0,2:T(2,128)(2,1)} %copy.78), calls=%async_computation.2 | async-start | bytes 3145728 | tf_op jit(solution)/shard_map/all_to_all | solution.py:262
  435.2 270.0 %reduce-scatter.14.cloned.1.call-start = ((), (), s32[]{:S(2)}) async-start(), calls=%async_computation.21 | async-start | bytes 5308416 | tf_op jit(solution)/shard_map/reduce_scatter | solution.py:302
  442.3 262.8 %reduce-scatter.10.cloned.1.call-start = ((), (), s32[]{:S(2)}) async-start(), calls=%async_computation.19 | async-start | bytes 2654208 | tf_op jit(solution)/shard_map/reduce_scatter | solution.py:296
  472.6 7.6 copy-start.37
  491.0 10.2 copy-start.4
  507.3 8.3 copy-start.3
  527.4 10.0 copy-start.4
  543.6 8.3 copy-start.3
  655.4 86.8 %reduce-scatter.12.cloned.1.call-start = ((), (), s32[]{:S(2)}) async-start(), calls=%async_computation.20 | async-start | bytes 2654208 | tf_op jit(solution)/shard_map/reduce_scatter | solution.py:299
  659.9 139.6 %reduce-scatter.8.cloned.1.call-start = ((), (), s32[]{:S(2)}) async-start(), calls=%async_computation.18 | async-start | bytes 5308416 | tf_op jit(solution)/shard_map/reduce_scatter | solution.py:293
  666.5 228.7 %reduce-scatter.16.cloned.1.call-start = ((), (), s32[]{:S(2)}) async-start(), calls=%async_computation.22 | async-start | bytes 14155776 | tf_op jit(solution)/shard_map/reduce_scatter | solution.py:244
  679.8 311.2 %reduce-scatter.18.cloned.1.call-start = ((), (), s32[]{:S(2)}) async-start(), calls=%async_computation.23 | async-start | bytes 14155776 | tf_op jit(solution)/shard_map/reduce_scatter | solution.py:247
  691.7 394.9 %reduce-scatter.20.cloned.1.call-start = ((), (), s32[]{:S(2)}) async-start(), calls=%async_computation.24 | async-start | bytes 14155776 | tf_op jit(solution)/shard_map/reduce_scatter | solution.py:250
  705.0 614.0 %all-reduce.10.cloned.1.call-start = ((), (), s32[]{:S(2)}) async-start(), calls=%async_computation.25 | async-start | bytes 12976128 | tf_op jit(solution)/shard_map/psum | solution.py:309
  1088.5 12.2 copy-start.19
  (32 other events, 85.5 us)
Sparse Core Ops, SparseCore 0:
  9.9 31.8 all-gather.9
  43.6 28.8 all-gather.11
  74.4 38.7 all-gather.7
  115.0 38.7 all-gather.13
  155.5 71.9 all-gather.15
  229.3 71.9 all-gather.17
  303.2 71.9 all-gather.19
  442.5 54.2 reduce-scatter.13
  655.5 40.4 reduce-scatter.9
  699.8 42.3 reduce-scatter.11
  745.7 53.7 reduce-scatter.7
  802.8 92.2 reduce-scatter.15
  898.7 92.2 reduce-scatter.17
  994.3 92.2 reduce-scatter.19
  1089.4 229.5 all-reduce.9
where the time goes:
time: 1340 us
  waiting for transfers between devices  810 us (60%)
  matrix products  249 us (19%)
  blocking collectives  115 us (9%)
  local copies, waits for them, and re-layouts  89.6 us (7%)
  other arithmetic  42.4 us (3%)
  between operations  16.2 us (1%)
  starting transfers between devices  14.4 us (1%)
    psum x1, waiting for transfers between devices, body(): lax.psum(attn_shards[1].astype(jnp.bfloat16), 'seq').astype(jnp.float32)  175 us
    reduce_scatter x1, waiting for transfers between devices, body(): lax.psum_scatter(grad_up.astype(jnp.bfloat16), 'fsdp', scatter_dimension=...  95.8 us
    reduce_scatter x1, waiting for transfers between devices, body(): lax.psum_scatter(grad_gate.astype(jnp.bfloat16), 'fsdp', scatter_dimensio...  95.7 us
    reduce_scatter x1, waiting for transfers between devices, body(): lax.psum_scatter(grad_down.astype(jnp.bfloat16), 'fsdp', scatter_dimensio...  95.7 us
    all_to_all x1, blocking collectives, body(): lax.all_to_all(packed_grads, 'seq', split_axis=1, concat_axis=2, tiled=True)  73.6 us
    all_to_all x1, waiting for transfers between devices, body(): lax.all_to_all(packed_arrays, 'seq', split_axis=2, concat_axis=1, tiled=T...  71.1 us
    reduce_scatter x1, waiting for transfers between devices, body(): lax.psum_scatter(grad_query.astype(jnp.bfloat16), 'fsdp', scatter_dimensi...  57.3 us
    all_gather x1, waiting for transfers between devices, body(): lax.all_gather(down_weight, 'fsdp', axis=0, tiled=True)  46.9 us
  transfers between devices with their start and end apart: 18, of which 13 were waited for; matrix products, arithmetic and copies ran while one was open for 22% of the time, Pallas kernels for 0%

commit v1 on v0

--- a/solution.py
+++ b/solution.py
@@ -11,6 +11,32 @@
 norm_eps = 1e-05
 rope_base = 100000.0
 masked_score = -1e30
+
+
+def _close_space(payload, dim_k, panel):
+    r_now = payload.shape
+    earlier = payload.reshape(*r_now[:dim_k], panel, r_now[dim_k] // panel, *r_now[dim_k + 1 :])
+    local_part = jnp.moveaxis(earlier, dim_k, 0)
+    return local_part
+
+
+def get_levels_all_in(xin, where_dim):
+    seen_now = list(xin.shape[1:])
+    seen_now[where_dim] *= xin.shape[0]
+    answer = jnp.moveaxis(xin, 0, where_dim).reshape(seen_now)
+    return answer
+
+
+def review_tiles(x0, which_axis, load, field_in):
+    row_out, item_now = (jax.lax.axis_size(which_axis), jax.lax.axis_index(which_axis))
+    current_block = _close_space(x0, load, row_out)
+    ledger = [current_block[item_now]]
+    for at in range(1, row_out):
+        z1 = current_block[item_now ^ at]
+        ledger.append(jax.lax.ppermute(z1, which_axis, [(k0, k0 ^ at) for k0 in range(row_out)]))
+    current_block = jnp.stack(ledger)[item_now ^ jnp.arange(row_out)]
+    now = get_levels_all_in(current_block, field_in)
+    return now
 
 
 def rope_tables(positions, head_size):
@@ -188,9 +214,7 @@
         sequence_count, span_length, KEY_VALUE_HEADS * (group_size + 2) * HEAD_DIM
     )
     attend_fn = partial(attend_items, group_size=group_size, head_size=HEAD_DIM)
-    heads_attended, log_totals, head_inputs = attend_fn(
-        lax.all_to_all(packed_arrays, "seq", split_axis=2, concat_axis=1, tiled=True)
-    )
+    heads_attended, log_totals, head_inputs = attend_fn(review_tiles(packed_arrays, "seq", 2, 1))
     attended_flat = lax.all_to_all(
         heads_attended, "seq", split_axis=1, concat_axis=2, tiled=True
     ).reshape(row_count, QUERY_HEADS * HEAD_DIM)

time: 1340 us -> 1350 us (level)
  waiting for transfers between devices: 810 us -> 778 us
  local copies, waits for them, and re-layouts: 89.6 us -> 104 us
  starting transfers between devices: 14.4 us -> 28.7 us
    all_to_all x1 -> x0, waiting for transfers between devices: 71.1 us -> none  [body(): lax.all_to_all(packed_arrays, 'seq', split_axis=2, concat_axis=1, tiled=T...]
    ppermute x0 -> x3, waiting for transfers between devices: none -> 48.6 us  [review_tiles(): jax.lax.ppermute(z1, which_axis, [(k0, k0 ^ at) for k0 in range(row_out)])]
    all_to_all x1, starting transfers between devices: 4.58 us -> 19.1 us  [body(): lax.all_to_all(heads_attended, 'seq', split_axis=1, concat_axis=2, tiled=...]
  transfers between devices with their start and end apart: 18 -> 20, of which waited for: 13 -> 14; matrix products, arithmetic and copies ran while one was open for 22% -> 24% of each run, Pallas kernels for 0% -> 0%
where the time goes in v1:
time: 1350 us; the launch traced here: 1340 us
  waiting for transfers between devices  778 us (58%)
  matrix products  249 us (18%)
  blocking collectives  115 us (9%)
  local copies, waits for them, and re-layouts  104 us (8%)
  other arithmetic  46 us (3%)
  starting transfers between devices  28.7 us (2%)
  between operations  16.3 us (1%)
    psum x1, waiting for transfers between devices, body(): lax.psum(attn_shards[1].astype(jnp.bfloat16), 'seq').astype(jnp.float32)  174 us
    reduce_scatter x1, waiting for transfers between devices, body(): lax.psum_scatter(grad_up.astype(jnp.bfloat16), 'fsdp', scatter_dimension=...  95.8 us
    reduce_scatter x1, waiting for transfers between devices, body(): lax.psum_scatter(grad_down.astype(jnp.bfloat16), 'fsdp', scatter_dimensio...  95.7 us
    reduce_scatter x1, waiting for transfers between devices, body(): lax.psum_scatter(grad_gate.astype(jnp.bfloat16), 'fsdp', scatter_dimensio...  95.7 us
    all_to_all x1, blocking collectives, body(): lax.all_to_all(packed_grads, 'seq', split_axis=1, concat_axis=2, tiled=True)  73.5 us
    reduce_scatter x1, waiting for transfers between devices, body(): lax.psum_scatter(grad_query.astype(jnp.bfloat16), 'fsdp', scatter_dimensi...  57.3 us
    ppermute x3, waiting for transfers between devices, review_tiles(): jax.lax.ppermute(z1, which_axis, [(k0, k0 ^ at) for k0 in range(row_out)])  48.6 us
    all_gather x1, waiting for transfers between devices, body(): lax.all_gather(down_weight, 'fsdp', axis=0, tiled=True)  37.4 us
  transfers between devices with their start and end apart: 20, of which 14 were waited for; matrix products, arithmetic and copies ran while one was open for 24% of the time, Pallas kernels for 0%

profile of v1, /device:TPU:0, one launch (start us, length us, event | category | flops | bytes accessed | tf_op | source)
XLA Modules:
  0.0 1337.3 jit_solution(18415690330121915946)
XLA Ops:
  13.8 15.5 %all-reduce.5 = (bf16[1536]{0:T(1024)(128)(2,1)S(1)}, bf16[1536]{0:T(1024)(128)(2,1)S(1)}) all-reduce(bf16[1536]{0:T(1024)(128)(2,1)S(1)} %dynamic-update-slice, bf16[1536]{0:T(1024)(128)(2,1)S(1)} %dynamic-update-slice.1), channel_id=1, replica_groups=mesh['seq'=4,'fsdp'=8] {'fsdp'}, use_global_device_ids=true, to_apply=%add | all-reduce | flops 3072 | bytes 12288
  44.6 28.0 %all-gather.12.cloned.1.call-done = bf16[1536,768]{1,0:T(8,128)(2,1)} async-done(((bf16[192,768]{1,0:T(8,128)(2,1)}), bf16[1536,768]{1,0:T(8,128)(2,1)}) %all-gather.12.cloned.1.call-update) | async-done | bytes 2359312 | tf_op jit(solution)/shard_map/all_gather | solution.py:173
  81.5 31.7 %all-gather.8.cloned.1.call-done = bf16[1536,1536]{1,0:T(8,128)(2,1)} async-done(((bf16[192,1536]{1,0:T(8,128)(2,1)}), bf16[1536,1536]{1,0:T(8,128)(2,1)}) %all-gather.8.cloned.1.call-update) | async-done | bytes 4718608 | tf_op jit(solution)/shard_map/all_gather | solution.py:171
  148.2 22.5 %collective-permute-done = bf16[2,256,768]{2,1,0:T(8,128)(2,1)S(1)} collective-permute-done((bf16[2,256,768]{2,1,0:T(8,128)(2,1)}, bf16[2,256,768]{2,1,0:T(8,128)(2,1)S(1)}, u32[]{:S(2)}, u32[]{:S(2)}) %collective-permute-start) | collective-permute-done | bytes 786464 | tf_op jit(solution)/shard_map/ppermute | solution.py:36
  170.7 26.1 %collective-permute-done.1 = bf16[2,256,768]{2,1,0:T(8,128)(2,1)S(1)} collective-permute-done((bf16[2,256,768]{2,1,0:T(8,128)(2,1)}, bf16[2,256,768]{2,1,0:T(8,128)(2,1)S(1)}, u32[]{:S(2)}, u32[]{:S(2)}) %collective-permute-start.1) | collective-permute-done | bytes 786464 | tf_op jit(solution)/shard_map/ppermute | solution.py:36
  209.4 29.2 %while.25 = (s32[]{:T(128)}, bf16[2,1024,384]{1,2,0:T(8,128)(2,1)}, f32[2,2,2,1024]{3,2,1,0:T(2,128)S(1)}, bf16[2,1024,768]{1,2,0:T(8,128)(2,1)S(1)}, s32[]{:T(128)}) while((s32[]{:T(128)}, bf16[2,1024,384]{1,2,0:T(8,128)(2,1)}, f32[2,2,2,1024]{3,2,1,0:T(2,128)S(1)}, bf16[2,1024,768]{1,2,0:T(8,128)(2,1)S(1)}, s32[]{:T(128)}) %tuple.83), condition=%wide.region_4.5_spmd, body=%wide.region_1.4_spmd.sunk | while | flops 1658187776 | bytes 68026976 | solution.py:103
  243.6 19.1 %all-to-all-start = ((bf16[2,1024,384]{2,0,1:T(2,128)(2,1)}), bf16[2,1024,384]{2,0,1:T(2,128)(2,1)}, u32[]{:S(2)}, u32[]{:S(2)}) async-start(bf16[2,1024,384]{2,0,1:T(2,128)(2,1)} %copy.86), calls=%async_computation | async-start | bytes 3145728 | tf_op jit(solution)/shard_map/all_to_all | solution.py:218
  266.9 33.0 %all-to-all-done = bf16[2,1024,384]{2,0,1:T(2,128)(2,1)} async-done(((bf16[2,1024,384]{2,0,1:T(2,128)(2,1)}), bf16[2,1024,384]{2,0,1:T(2,128)(2,1)}, u32[]{:S(2)}, u32[]{:S(2)}) %all-to-all-start) | async-done | bytes 1572896 | tf_op jit(solution)/shard_map/all_to_all | solution.py:218
  313.6 12.1 fusion.47
  325.7 12.2 fusion.48
  337.9 37.4 %all-gather.20.cloned.1.call-done = bf16[4096,1536]{1,0:T(8,128)(2,1)} async-done(((bf16[512,1536]{1,0:T(8,128)(2,1)}), bf16[4096,1536]{1,0:T(8,128)(2,1)}) %all-gather.20.cloned.1.call-update) | async-done | bytes 12582928 | tf_op jit(solution)/shard_map/all_gather | solution.py:237
  375.2 19.2 %multiply_convert_fusion = (bf16[512,4096]{1,0:T(8,128)(2,1)}, bf16[512,4096]{1,0:T(8,128)(2,1)}, bf16[512,4096]{1,0:T(8,128)(2,1)}) fusion(f32[512,4096]{1,0:T(8,128)} %fusion.47, f32[512,4096]{1,0:T(8,128)} %fusion.48, bf16[512,1536]{1,0:T(8,128)(2,1)} %bitcast_convert_fusion, bf16[4096,1536]{1,0:T(8,128)(2,1)} %all-gather.20.cloned.1.call-done), kind=kOutput, calls=%fused_computation.62 | convolution fusion | flops 6476005376 | bytes 43515904 | tf_op jit(solution)/shard_map/dot_general | solution.py:244
  394.4 10.9 fusion.49
  405.4 12.0 multiply_reduce_fusion
  442.1 30.2 %all-to-all-done.1 = bf16[2,256,1536]{1,0,2:T(2,128)(2,1)} async-done(((bf16[2,256,1536]{1,0,2:T(2,128)(2,1)}), bf16[2,256,1536]{1,0,2:T(2,128)(2,1)}, u32[]{:S(2)}, u32[]{:S(2)}) %all-to-all-start.1) | async-done | bytes 1572896 | tf_op jit(solution)/shard_map/all_to_all | solution.py:286
  480.0 73.4 %while.26 = (s32[]{:T(128)}, bf16[2,1024,768]{1,2,0:T(8,128)(2,1)}, bf16[2,1024,768]{1,2,0:T(8,128)(2,1)S(1)}, f32[2,2,2,1024]{3,2,1,0:T(2,128)S(1)}, bf16[2,102...) while((s32[]{:T(128)}, bf16[2,1024,768]{1,2,0:T(8,128)(2,1)}, ...), condition=%wide.region_8.9_spmd.clone.clone.clone, body=%wide.region_7.8_spmd.clone.clone.clone.sunk | while | flops 4085755904 | bytes 115446648 | solution.py:292
  491.0 10.1 fusion.122
  527.3 10.0 fusion.122
  561.0 73.5 %all_to_all.48 = bf16[2,1024,768]{2,0,1:T(2,128)(2,1)} all-to-all(bf16[2,1024,768]{2,0,1:T(2,128)(2,1)S(1)} %copy.91), channel_id=1, replica_groups=mesh['seq'=4,'fsdp'=8] {'seq'}, dimensions={1} | all-to-all | bytes 6291456 | tf_op jit(solution)/shard_map/all_to_all | solution.py:293
  634.6 11.2 copy.92
  667.6 11.8 convolution_convert_fusion.2
  679.5 11.9 convolution_convert_fusion.1
  692.8 12.1 convolution_convert_fusion
  705.0 36.9 %reduce-scatter.12.cloned.1.call-done = bf16[192,768]{1,0:T(8,128)(2,1)} async-done(((bf16[1536,768]{1,0:T(8,128)(2,1)}), bf16[192,768]{1,0:T(8,128)(2,1)}) %reduce-scatter.12.cloned.1.call-update) | async-done | bytes 294928 | tf_op jit(solution)/shard_map/reduce_scatter | solution.py:323
  741.9 57.3 %reduce-scatter.8.cloned.1.call-done = bf16[192,1536]{1,0:T(8,128)(2,1)} async-done(((bf16[1536,1536]{1,0:T(8,128)(2,1)}), bf16[192,1536]{1,0:T(8,128)(2,1)}) %reduce-scatter.8.cloned.1.call-update) | async-done | bytes 589840 | tf_op jit(solution)/shard_map/reduce_scatter | solution.py:317
  799.2 95.7 %reduce-scatter.16.cloned.1.call-done = bf16[192,4096]{1,0:T(8,128)(2,1)} async-done(((bf16[1536,4096]{1,0:T(8,128)(2,1)}), bf16[192,4096]{1,0:T(8,128)(2,1)}) %reduce-scatter.16.cloned.1.call-update) | async-done | bytes 1572880 | tf_op jit(solution)/shard_map/reduce_scatter | solution.py:268
  894.8 95.8 %reduce-scatter.18.cloned.1.call-done = bf16[192,4096]{1,0:T(8,128)(2,1)} async-done(((bf16[1536,4096]{1,0:T(8,128)(2,1)}), bf16[192,4096]{1,0:T(8,128)(2,1)}) %reduce-scatter.18.cloned.1.call-update) | async-done | bytes 1572880 | tf_op jit(solution)/shard_map/reduce_scatter | solution.py:271
  990.6 95.7 %reduce-scatter.20.cloned.1.call-done = bf16[512,1536]{1,0:T(8,128)(2,1)} async-done(((bf16[4096,1536]{1,0:T(8,128)(2,1)}), bf16[512,1536]{1,0:T(8,128)(2,1)}) %reduce-scatter.20.cloned.1.call-update) | async-done | bytes 1572880 | tf_op jit(solution)/shard_map/reduce_scatter | solution.py:274
  1088.2 12.3 convolution_add_fusion.3
  1111.8 13.6 %all-reduce.4 = (bf16[1536]{0:T(1024)(128)(2,1)S(1)}, bf16[1536]{0:T(1024)(128)(2,1)S(1)}) all-reduce(bf16[1536]{0:T(1024)(128)(2,1)S(1)} %get-tuple-element.208, bf16[1536]{0:T(1024)(128)(2,1)S(1)} %copy-done.40), channel_id=2, replica_groups=mesh['seq'=4,'fsdp'=8] {'fsdp'}, use_global_device_ids=true, to_apply=%region_11.12.clone | all-reduce | flops 3072 | bytes 12288
  1125.5 12.3 all-reduce.6
  1144.3 174.4 %all-reduce.10.cloned.1.call-done = (bf16[192,1536]{1,0:T(8,128)(2,1)}, bf16[192,768]{1,0:T(8,128)(2,1)}, bf16[192,768]{1,0:T(8,128)(2,1)}, bf16[192,1536]{1,0:T...) async-done(((bf16[192,1536]{1,0:T(8,128)(2,1)}, bf16[192,768]{1,0:T(8,128)(2,1)}, bf16[192,768]{1,0:T(8,128)(2,1)}, ...) | async-done | bytes 6488080 | tf_op jit(solution)/shard_map/psum | solution.py:333
  (261 shorter events, 275.4 us)
Async XLA Ops:
  7.2 34.6 %all-gather.10.cloned.1.call-start = ((), (), s32[]{:S(2)}) async-start(), calls=%async_computation.11 | async-start | bytes 2654208 | tf_op jit(solution)/shard_map/all_gather | solution.py:172
  7.9 64.6 %all-gather.12.cloned.1.call-start = ((), (), s32[]{:S(2)}) async-start(), calls=%async_computation.12 | async-start | bytes 2654208 | tf_op jit(solution)/shard_map/all_gather | solution.py:173
  8.7 104.5 %all-gather.8.cloned.1.call-start = ((), (), s32[]{:S(2)}) async-start(), calls=%async_computation.10 | async-start | bytes 5308416 | tf_op jit(solution)/shard_map/all_gather | solution.py:171
  9.4 20.5 %copy-start = (f32[2,256,1536]{2,1,0:T(8,128)S(1)}, f32[2,256,1536]{2,1,0:T(8,128)}, u32[]{:S(2)}) copy-start(f32[2,256,1536]{2,1,0:T(8,128)} %param.15) | copy-start | bytes 9437188
  9.4 294.5 %all-gather.14.cloned.1.call-start = ((), (), s32[]{:S(2)}) async-start(), calls=%async_computation.13 | async-start | bytes 5308416 | tf_op jit(solution)/shard_map/all_gather | solution.py:174
  10.0 303.5 %all-gather.16.cloned.1.call-start = ((), (), s32[]{:S(2)}) async-start(), calls=%async_computation.14 | async-start | bytes 14155776 | tf_op jit(solution)/shard_map/all_gather | solution.py:226
  10.6 315.1 %all-gather.18.cloned.1.call-start = ((), (), s32[]{:S(2)}) async-start(), calls=%async_computation.15 | async-start | bytes 14155776 | tf_op jit(solution)/shard_map/all_gather | solution.py:227
  11.2 364.1 %all-gather.20.cloned.1.call-start = ((), (), s32[]{:S(2)}) async-start(), calls=%async_computation.16 | async-start | bytes 14155776 | tf_op jit(solution)/shard_map/all_gather | solution.py:237
  134.0 10.0 copy-start.16
  134.0 12.4 copy-start.15
  137.2 33.5 %collective-permute-start = (bf16[2,256,768]{2,1,0:T(8,128)(2,1)}, bf16[2,256,768]{2,1,0:T(8,128)(2,1)S(1)}, u32[]{:S(2)}, u32[]{:S(2)}) collective-permute-start(bf16[2,256,768]{2,1,0:T(8,128)(2,1)} %bitcast.30), channel_id=1, source_target_pairs={{0,8},{8,0},{16,24},{24,16},{1,9},{9,1},{17,25},{25,17},{2,10},{10... | collective-permute-start | bytes 2359304 | tf_op jit(solution)/shard_map/ppermute | solution.py:36
  141.6 55.2 %collective-permute-start.1 = (bf16[2,256,768]{2,1,0:T(8,128)(2,1)}, bf16[2,256,768]{2,1,0:T(8,128)(2,1)S(1)}, u32[]{:S(2)}, u32[]{:S(2)}) collective-permute-start(bf16[2,256,768]{2,1,0:T(8,128)(2,1)} %bitcast.335), channel_id=1, source_target_pairs={{0,16},{8,24},{16,0},{24,8},{1,17},{9,25},{17,1},{25,9},{2,18},{10... | collective-permute-start | bytes 2359304 | tf_op jit(solution)/shard_map/ppermute | solution.py:36
  145.8 51.1 %collective-permute-start.2 = (bf16[2,256,768]{2,1,0:T(8,128)(2,1)}, bf16[2,256,768]{2,1,0:T(8,128)(2,1)S(1)}, u32[]{:S(2)}, u32[]{:S(2)}) collective-permute-start(bf16[2,256,768]{2,1,0:T(8,128)(2,1)} %bitcast.336), channel_id=1, source_target_pairs={{0,24},{8,16},{16,8},{24,0},{1,25},{9,17},{17,9},{25,1},{2,26},{10... | collective-permute-start | bytes 2359304 | tf_op jit(solution)/shard_map/ppermute | solution.py:36
  170.7 26.2 %copy-start.27 = (bf16[2,256,768]{2,1,0:T(8,128)(2,1)}, bf16[2,256,768]{2,1,0:T(8,128)(2,1)S(1)}, u32[]{:S(2)}) copy-start(bf16[2,256,768]{2,1,0:T(8,128)(2,1)S(1)} %collective-permute-done) | copy-start | bytes 2359300
  243.6 56.3 %all-to-all-start = ((bf16[2,1024,384]{2,0,1:T(2,128)(2,1)}), bf16[2,1024,384]{2,0,1:T(2,128)(2,1)}, u32[]{:S(2)}, u32[]{:S(2)}) async-start(bf16[2,1024,384]{2,0,1:T(2,128)(2,1)} %copy.86), calls=%async_computation | async-start | bytes 3145728 | tf_op jit(solution)/shard_map/all_to_all | solution.py:218
  394.4 10.9 copy-start.9
  405.4 12.0 copy-start.6
  430.3 42.1 %all-to-all-start.1 = ((bf16[2,256,1536]{1,0,2:T(2,128)(2,1)}), bf16[2,256,1536]{1,0,2:T(2,128)(2,1)}, u32[]{:S(2)}, u32[]{:S(2)}) async-start(bf16[2,256,1536]{1,0,2:T(2,128)(2,1)} %copy.88), calls=%async_computation.1 | async-start | bytes 3145728 | tf_op jit(solution)/shard_map/all_to_all | solution.py:286
  434.9 270.1 %reduce-scatter.14.cloned.1.call-start = ((), (), s32[]{:S(2)}) async-start(), calls=%async_computation.20 | async-start | bytes 5308416 | tf_op jit(solution)/shard_map/reduce_scatter | solution.py:326
  442.1 262.9 %reduce-scatter.10.cloned.1.call-start = ((), (), s32[]{:S(2)}) async-start(), calls=%async_computation.18 | async-start | bytes 2654208 | tf_op jit(solution)/shard_map/reduce_scatter | solution.py:320
  472.4 7.6 copy-start.39
  491.0 10.1 copy-start.4
  507.3 8.3 copy-start.3
  527.3 10.1 copy-start.4
  543.5 8.3 copy-start.3
  655.1 86.8 %reduce-scatter.12.cloned.1.call-start = ((), (), s32[]{:S(2)}) async-start(), calls=%async_computation.19 | async-start | bytes 2654208 | tf_op jit(solution)/shard_map/reduce_scatter | solution.py:323
  659.6 139.5 %reduce-scatter.8.cloned.1.call-start = ((), (), s32[]{:S(2)}) async-start(), calls=%async_computation.17 | async-start | bytes 5308416 | tf_op jit(solution)/shard_map/reduce_scatter | solution.py:317
  666.2 228.7 %reduce-scatter.16.cloned.1.call-start = ((), (), s32[]{:S(2)}) async-start(), calls=%async_computation.21 | async-start | bytes 14155776 | tf_op jit(solution)/shard_map/reduce_scatter | solution.py:268
  679.4 311.2 %reduce-scatter.18.cloned.1.call-start = ((), (), s32[]{:S(2)}) async-start(), calls=%async_computation.22 | async-start | bytes 14155776 | tf_op jit(solution)/shard_map/reduce_scatter | solution.py:271
  691.4 394.9 %reduce-scatter.20.cloned.1.call-start = ((), (), s32[]{:S(2)}) async-start(), calls=%async_computation.23 | async-start | bytes 14155776 | tf_op jit(solution)/shard_map/reduce_scatter | solution.py:274
  704.9 613.8 %all-reduce.10.cloned.1.call-start = ((), (), s32[]{:S(2)}) async-start(), calls=%async_computation.24 | async-start | bytes 12976128 | tf_op jit(solution)/shard_map/psum | solution.py:333
  1088.2 12.3 copy-start.19
  (36 other events, 106.8 us)
Sparse Core Ops, SparseCore 0:
  9.9 31.8 all-gather.9
  43.6 28.8 all-gather.11
  74.4 38.7 all-gather.7
  115.0 38.7 all-gather.13
  155.5 71.9 all-gather.15
  229.3 71.9 all-gather.17
  303.2 71.9 all-gather.19
  442.2 54.2 reduce-scatter.13
  655.2 40.4 reduce-scatter.9
  699.5 42.3 reduce-scatter.11
  745.3 53.7 reduce-scatter.7
  802.5 92.2 reduce-scatter.15
  898.3 92.2 reduce-scatter.17
  994.0 92.2 reduce-scatter.19
  1089.1 229.5 all-reduce.9
